TPU v7x, 32 devices: a whole 2x2x4 slice. The times are simulated.
32 devices in a mesh: param: 16 (over z, x, core), qoi: 2 (over y).
Axes of the slice: x: 2, y: 2, z: 4, core: 2. Of those that a mesh axis runs over, the one named last changes fastest.
Arguments:
- samples: bfloat16 [16, 5120, 420], P('qoi', 'param'), may hold values from -6 to 6
- operator_rows: bfloat16 [8, 5120, 2, 512], P(None, 'param', None, 'qoi'), may hold values from -0.0625 to 0.0625
- block_start: int32 [1], replicated, may hold values from 0 to 203
- gauge_group: int32 [512], P('qoi'), may hold values from 0 to 15
Outputs:
- qoi_spectrum: float32 [16, 2, 8, 512], P('param', None, None, 'qoi')
- segment_response: float32 [16, 2, 8, 16], P('param')
Inputs may be any that keep to these rules, and one draw needn't show every extreme that they name: `block_start`: the block's frequencies lie among the 211 frequencies of a real transform.
All inputs are finite; a program needn't handle non-finite values.
Results may differ from a plain program's by a relative error of at most 0.005.
Values may be sent and summed in bfloat16 or wider, within the bound.
No kernel may reach another device: no remote copies, remote signals or barrier semaphores. Data moves between devices by JAX's collectives and lax.ppermute only.
A program may use at most 64 MiB of HBM per device.

v0:
```python
import math

import jax
import jax.numpy as jnp
from jax import lax
from jax.sharding import PartitionSpec as P

GROUPS = 16


def build_table(block_start, steps_count, freq_count):
    time_index = jnp.arange(steps_count, dtype=jnp.int32)
    freq_index = block_start[0] + jnp.arange(freq_count, dtype=jnp.int32)
    phase_index = time_index[:, None] * freq_index[None, :] % steps_count
    phases = phase_index.astype(jnp.float32) * (2.0 * math.pi / steps_count)
    table = jnp.concatenate([jnp.cos(phases), -jnp.sin(phases)], axis=1) / math.sqrt(steps_count)
    table_high = lax.optimization_barrier(table.astype(jnp.bfloat16))
    table_low = (table - table_high.astype(jnp.float32)).astype(jnp.bfloat16)
    return jnp.concatenate([table_high, table_low], axis=1)


def transform(series, combined, freq_count):
    sample_count, param_local, steps_count = series.shape
    flat = series.reshape(sample_count * param_local, steps_count)
    halves = jnp.dot(flat, combined, preferred_element_type=jnp.float32)
    spectrum = (halves[:, : 2 * freq_count] + halves[:, 2 * freq_count :]).astype(jnp.bfloat16)
    return spectrum.reshape(sample_count, param_local, 2, freq_count).transpose(3, 2, 0, 1)


def local(samples, operator_rows, block_start, gauge_group):
    freq_count = operator_rows.shape[0]
    param_local = operator_rows.shape[1]
    gauge_local = operator_rows.shape[3]
    combined = build_table(block_start, samples.shape[2], freq_count)
    spectra = lax.all_gather(transform(samples, combined, freq_count), "qoi", axis=2, tiled=True)
    sample_total = spectra.shape[2]
    weights = operator_rows.reshape(freq_count, param_local, 2 * gauge_local)
    param_count = lax.axis_size("param")
    own_rows = sample_total // param_count
    product = jnp.einsum("fkcp,fpx->ckfx", spectra, weights, preferred_element_type=jnp.float32)
    real_part = product[:, 0, :, :gauge_local] - product[:, 1, :, gauge_local:]
    imag_part = product[:, 0, :, gauge_local:] + product[:, 1, :, :gauge_local]
    all_terms = jnp.stack([real_part, imag_part], axis=1)
    received = lax.all_to_all(
        all_terms.astype(jnp.bfloat16), "param", split_axis=0, concat_axis=0, tiled=True
    ).astype(all_terms.dtype)
    qoi_spectrum = jnp.sum(
        received.reshape(param_count, own_rows, 2, freq_count, gauge_local), axis=0
    )
    onehot = (gauge_group[:, None] == jnp.arange(GROUPS, dtype=jnp.int32)[None, :]).astype(
        jnp.float32
    )
    local_sums = jnp.dot(
        qoi_spectrum.reshape(-1, gauge_local),
        onehot,
        precision=lax.Precision.HIGHEST,
        preferred_element_type=jnp.float32,
    )
    local_sums = local_sums.reshape(own_rows, 2, freq_count, GROUPS)
    summed = lax.psum(local_sums, "qoi")
    norm_factor = math.sqrt(GROUPS / (gauge_local * lax.axis_size("qoi")))
    return (qoi_spectrum, summed * norm_factor)


def solution(mesh):
    return jax.shard_map(
        local,
        mesh=mesh,
        in_specs=(P("qoi", "param", None), P(None, "param", None, "qoi"), P(), P("qoi")),
        out_specs=(P("param", None, None, "qoi"), P("param", None, None, None)),
        check_vma=False,
    )
```

profile of v0, /device:TPU:0, one launch (start us, length us, event | category | flops | bytes accessed | tf_op | source)
XLA Modules:
  0.0 37.9 jit_solution(8787217125666526188)
XLA Ops:
  1.3 0.2 fusion.16
  1.5 4.1 %reshape.28 = bf16[2560,420]{0,1:T(8,128)(2,1)S(1)} reshape(bf16[8,320,420]{1,0,2:T(8,128)(2,1)} %param.4) | data formatting | bytes 4300800 | tf_op jit(solution)/shard_map/reshape | solution.py:24
  5.6 0.5 %convolution_bitcast_fusion = f32[2560,32]{0,1:T(8,128)S(1)} fusion(bf16[2560,420]{0,1:T(8,128)(2,1)S(1)} %reshape.28, bf16[420,16]{0,1:T(8,128)(2,1)S(1)} %subtract_convert_fusion, bf16[420,16]{0,1:T(8,128)(2,1)S(1)} %fusion.11), kind=kOutput, calls=%fused_computation | convolution fusion | flops 68866560 | bytes 2504960 | tf_op jit(solution)/shard_map/dot_general | solution.py:25
  6.1 0.1 reshape.29
  6.2 6.5 %all_gather.3 = bf16[8,2,16,320]{3,2,1,0:T(8,128)(2,1)S(1)} all-gather(bf16[8,2,8,320]{3,2,1,0:T(8,128)(2,1)S(1)} %bitcast.29), channel_id=1, replica_groups=mesh['param'=16,'qoi'=2] {'qoi'}, dimensions={2}, use_global_device_ids=true | all-gather | bytes 245760 | tf_op jit(solution)/shard_map/all_gather | solution.py:35
  12.7 4.2 %reshape.31 = bf16[8,320,512,1]{2,1,0,3:T(8,128)(2,1)S(1)} reshape(bf16[8,320,2,256]{3,2,1,0:T(2,128)(2,1)} %param.5) | data formatting | bytes 5242880 | tf_op jit(solution)/shard_map/reshape | solution.py:37
  16.9 0.0 copy-start
  16.9 0.5 %fusion.2 = f32[16,2,8,512]{3,0,1,2:T(8,128)S(1)} fusion(bf16[8,2,16,320]{3,2,1,0:T(8,128)(2,1)S(1)} %all_gather.3, bf16[8,320,512,1]{2,1,0,3:T(8,128)(2,1)S(1)} %reshape.31), kind=kOutput, calls=%fused_computation.3 | convolution fusion | flops 83886080 | bytes 3309568 | tf_op jit(solution)/shard_map/fkcp,fpx->ckfx/dot_general | solution.py:40
  17.5 0.1 copy.13
  17.6 13.9 %all_to_all.5 = bf16[16,2,8,256]{3,1,2,0:T(2,128)(2,1)S(1)} all-to-all(bf16[16,2,8,256]{3,1,2,0:T(2,128)(2,1)S(1)} %copy.13), channel_id=1, replica_groups=mesh['param'=16,'qoi'=2] {'param'}, dimensions={0} | all-to-all | bytes 262144 | tf_op jit(solution)/shard_map/all_to_all | solution.py:44
  31.6 0.0 copy-done
  31.6 0.1 convolution_bitcast_fusion.1
  31.7 0.6 %copy.17 = f32[1,2,8,256]{3,2,1,0:T(8,128)} copy(f32[1,2,8,256]{3,1,2,0:T(2,128)S(1)} %bitcast.30) | data formatting | bytes 32768
  32.3 5.0 %psum.7 = f32[1,2,8,16]{3,2,1,0:T(8,128)S(1)} all-reduce(f32[1,2,8,16]{3,2,1,0:T(8,128)S(1)} %convolution_bitcast_fusion.1), channel_id=1, replica_groups=mesh['param'=16,'qoi'=2] {'qoi'}, use_global_device_ids=true, to_apply=%region_1.2 | all-reduce | flops 256 | bytes 2048 | tf_op jit(solution)/shard_map/psum | solution.py:60
  37.3 0.6 %broadcast_multiply_fusion = f32[1,2,8,16]{3,2,1,0:T(8,128)} fusion(f32[1,2,8,16]{3,2,1,0:T(8,128)S(1)} %psum.7), kind=kLoop, calls=%fused_computation.33 | loop fusion | flops 256 | bytes 2048 | tf_op jit(solution)/shard_map/mul | solution.py:62
  (9 shorter events, 0.1 us)
Async XLA Ops:
  16.9 14.7 %copy-start = (s32[256]{0:T(256)S(1)}, s32[256]{0:T(256)}, u32[]{:S(2)}) copy-start(s32[256]{0:T(256)} %param.7) | copy-start | bytes 3076
where the time goes:
time: 38.2 us; the launch traced here: 37.9 us
  blocking collectives  25.3 us (66%)
  local copies, waits for them, and re-layouts  9.13 us (24%)
  between operations  1.38 us (4%)
  matrix products  1.14 us (3%)
  other arithmetic  0.88 us (2%)
    all_to_all x1, blocking collectives, local(): lax.all_to_all(all_terms.astype(jnp.bfloat16), 'param', split_axis=0, con...  13.9 us
    all_gather x1, blocking collectives, local(): lax.all_gather(transform(samples, combined, freq_count), 'qoi', axis=2, t...  6.46 us
    psum x1, blocking collectives, local(): summed = lax.psum(local_sums, 'qoi')  4.96 us
    reshape x1, local copies, waits for them, and re-layouts, local(): weights = operator_rows.reshape(freq_count, param_local, 2 * gauge_local)  4.16 us
    reshape x1, local copies, waits for them, and re-layouts, transform(): flat = series.reshape(sample_count * param_local, steps_count)  4.09 us

commit v1 on v0

v1 whole, which is shorter than its diff:
```python
import math

import jax
import jax.numpy as jnp
from jax import lax
from jax.experimental import pallas as pl
from jax.experimental.pallas import tpu as pltpu
from jax.sharding import PartitionSpec as P

GROUPS = 16
ROWS = 8


def build_table(block_start, steps_count, freq_count, series_count):
    column = jnp.arange(steps_count * series_count, dtype=jnp.int32) // series_count
    freq_index = block_start[0] + jnp.arange(freq_count, dtype=jnp.int32)
    phase_index = freq_index[:, None] * column[None, :] % steps_count
    phases = phase_index.astype(jnp.float32) * (2.0 * math.pi / steps_count)
    table = jnp.concatenate([jnp.cos(phases), -jnp.sin(phases)], axis=0) / math.sqrt(steps_count)
    table_high = lax.optimization_barrier(table.astype(jnp.bfloat16)).astype(jnp.float32)
    table_low = (table - table_high).astype(jnp.bfloat16).astype(jnp.float32)
    return jnp.concatenate([table_high, table_low], axis=0)


def transform_kernel(table_ref, series_ref, spectrum_ref, spread_ref):
    table_rows, columns = table_ref.shape
    series_count = spread_ref.shape[0] // table_rows
    shape = (series_count, columns)
    own = lax.broadcasted_iota(jnp.int32, shape, 1) % series_count == lax.broadcasted_iota(
        jnp.int32, shape, 0
    )
    for row in range(0, table_rows, 2):
        pair = [
            jnp.where(own, jnp.broadcast_to(table_ref[one : one + 1, :], shape), 0.0)
            for one in (row, row + 1)
        ]
        spread_ref[row * series_count : (row + 2) * series_count, :] = jnp.concatenate(
            pair, axis=0
        ).astype(jnp.bfloat16)
    halves = jnp.dot(spread_ref[...], series_ref[...], preferred_element_type=jnp.float32)
    half = halves.shape[0] // 2
    spectrum_ref[...] = (halves[:half] + halves[half:]).astype(jnp.bfloat16)


def transform(samples, block_start, freq_count):
    series_count, param_local, steps_count = samples.shape
    table = build_table(block_start, steps_count, freq_count, series_count)
    series = samples.transpose(2, 0, 1).reshape(steps_count * series_count, param_local)
    rows = 2 * freq_count * series_count
    return pl.pallas_call(
        transform_kernel,
        out_shape=jax.ShapeDtypeStruct((rows, param_local), jnp.bfloat16),
        scratch_shapes=[pltpu.VMEM((2 * rows, steps_count * series_count), jnp.bfloat16)],
        name="transform",
    )(table, series)


def product_kernel(place_ref, weights_ref, *refs):
    *spectra_refs, terms_ref, ordered_ref, stage_ref = refs
    freq_count, param_local, _, gauge_local = weights_ref.shape
    parts = len(spectra_refs)
    series_count = spectra_refs[0].shape[0] // (2 * freq_count)
    for step, ref in enumerate(spectra_refs):
        ordered_ref[lax.rem(place_ref[0] + step, parts)] = ref[...]
    shape = (param_local, 2 * param_local)
    double = (
        lax.broadcasted_iota(jnp.int32, shape, 1) // 2 == lax.broadcasted_iota(jnp.int32, shape, 0)
    )
    double = jnp.where(double, 1.0, 0.0).astype(jnp.bfloat16)
    spread = [
        jnp.dot(ordered_ref[part], double, preferred_element_type=jnp.float32)
        for part in range(parts)
    ]
    even = lax.broadcasted_iota(jnp.int32, (parts * series_count, 2 * param_local), 1) % 2 == 0
    for freq in range(freq_count):
        real, imag = [
            jnp.concatenate(
                [
                    one[(kind * freq_count + freq) * series_count :][:series_count]
                    for one in spread
                ],
                axis=0,
            )
            for kind in (0, 1)
        ]
        rows = jnp.concatenate(
            [jnp.where(even, real, -imag), jnp.where(even, imag, real)], axis=0
        ).astype(jnp.bfloat16)
        weights = weights_ref[freq].reshape(2 * param_local, gauge_local)
        product = jnp.dot(rows, weights, preferred_element_type=jnp.float32)
        half = parts * series_count
        stage_ref[:, 0, freq, :] = product[:half]
        stage_ref[:, 1, freq, :] = product[half:]
    terms_ref[...] = stage_ref[...].astype(jnp.bfloat16)


def exchange(own, axis):
    count = lax.axis_size(axis)
    moved = [own]
    for step in range(1, count):
        pairs = [(source, (source - step) % count) for source in range(count)]
        moved.append(lax.ppermute(own, axis, pairs))
    return moved


def products(spectrum, operator_rows):
    freq_count, param_local, _, gauge_local = operator_rows.shape
    spectra = exchange(spectrum, "qoi")
    place = lax.axis_index("qoi").astype(jnp.int32).reshape(1)
    samples_total = len(spectra) * spectrum.shape[0] // (2 * freq_count)
    shape = (samples_total, 2, freq_count, gauge_local)
    return pl.pallas_call(
        product_kernel,
        in_specs=[pl.BlockSpec(memory_space=pltpu.SMEM)]
        + [pl.BlockSpec(memory_space=pltpu.VMEM)] * (1 + len(spectra)),
        out_shape=jax.ShapeDtypeStruct(shape, jnp.bfloat16),
        scratch_shapes=[
            pltpu.VMEM((len(spectra),) + spectrum.shape, jnp.bfloat16),
            pltpu.VMEM(shape, jnp.float32),
        ],
        name="products",
    )(place, operator_rows, *spectra)


def scatter_sum(terms, stride, count):
    total = lax.axis_size("param")
    member = lax.axis_index("param") // stride % count
    moved = []
    for step in range(1, count):
        pairs = []
        for source in range(total):
            place = source // stride % count
            pairs.append((source, source + ((place + step) % count - place) * stride))
        chunk = lax.dynamic_index_in_dim(terms, (member + step) % count, 0, keepdims=False)
        moved.append(lax.ppermute(chunk.astype(jnp.bfloat16), "param", pairs))
    result = lax.dynamic_index_in_dim(terms, member, 0, keepdims=False).astype(jnp.float32)
    for one in moved:
        result = result + one.astype(jnp.float32)
    return result


def local(samples, operator_rows, block_start, gauge_group):
    freq_count = operator_rows.shape[0]
    gauge_local = operator_rows.shape[3]
    terms = products(transform(samples, block_start, freq_count), operator_rows)
    param_count = lax.axis_size("param")
    own_rows = terms.shape[0] // param_count
    inner = 4 if param_count % 4 == 0 else 1
    outer = param_count // inner
    rest = (own_rows, 2, freq_count, gauge_local)
    half_sums = scatter_sum(terms.reshape((outer, inner) + rest), inner, outer)
    qoi_spectrum = scatter_sum(half_sums, 1, inner)
    onehot = (gauge_group[:, None] == jnp.arange(GROUPS, dtype=jnp.int32)[None, :]).astype(
        jnp.float32
    )
    local_sums = jnp.dot(
        qoi_spectrum.reshape(-1, gauge_local),
        onehot,
        precision=lax.Precision.HIGHEST,
        preferred_element_type=jnp.float32,
    )
    local_sums = local_sums.reshape(own_rows, 2, freq_count, GROUPS)
    summed = sum(exchange(local_sums, "qoi"))
    norm_factor = math.sqrt(GROUPS / (gauge_local * lax.axis_size("qoi")))
    return (qoi_spectrum, summed * norm_factor)


def solution(mesh):
    return jax.shard_map(
        local,
        mesh=mesh,
        in_specs=(P("qoi", "param", None), P(None, "param", None, "qoi"), P(), P("qoi")),
        out_specs=(P("param", None, None, "qoi"), P("param", None, None, None)),
        check_vma=False,
    )
```

time: 38.2 us -> 37.5 us (0.982)
  blocking collectives: 25.3 us -> 0 us
  waiting for transfers between devices: 0 us -> 12.7 us
  starting transfers between devices: 0 us -> 11.3 us
  local copies, waits for them, and re-layouts: 9.13 us -> 1.46 us
  Pallas kernels: 0 us -> 7.32 us
  other arithmetic: 0.88 us -> 2.84 us
  matrix products: 1.14 us -> 0.12 us
    all_to_all x1 -> x0, blocking collectives: 13.9 us -> none  [local(): lax.all_to_all(all_terms.astype(jnp.bfloat16), 'param', split_axis=0, con...]
    ppermute x0 -> x8, waiting for transfers between devices: none -> 12.7 us  [the longest x6 7.62 us: scatter_sum(): moved.append(lax.ppermute(chunk.astype(jnp.bfloat16), 'param', pairs))]
    ppermute x0 -> x8, starting transfers between devices: none -> 11.3 us  [the longest x6 6.73 us: scatter_sum(): moved.append(lax.ppermute(chunk.astype(jnp.bfloat16), 'param', pairs))]
    reshape x4 -> x0, local copies, waits for them, and re-layouts: 8.39 us -> none  [the longest x1 4.16 us: local(): weights = operator_rows.reshape(freq_count, param_local, 2 * gauge_local)]
    pallas_call x0 -> x2, Pallas kernels: none -> 7.32 us  [the longest x1 3.72 us: products(): pl.pallas_call(product_kernel, in_specs=[pl.BlockSpec(memory_space=pltpu....]
    all_gather x1 -> x0, blocking collectives: 6.46 us -> none  [local(): lax.all_gather(transform(samples, combined, freq_count), 'qoi', axis=2, t...]
    psum x1 -> x0, blocking collectives: 4.96 us -> none  [local(): summed = lax.psum(local_sums, 'qoi')]
    dot_general x2 -> x0, matrix products: 1.02 us -> none  [the longest x1 0.54 us: local(): jnp.einsum('fkcp,fpx->ckfx', spectra, weights, preferred_element_type=jnp...]
  transfers between devices with their start and end apart: 0 -> 8, of which waited for: 0 -> 7; matrix products, arithmetic and copies ran while one was open for 0% -> 0% of each run, Pallas kernels for 0% -> 0%
where the time goes in v1:
time: 37.5 us; the launch traced here: 37.1 us
  waiting for transfers between devices  12.7 us (34%)
  starting transfers between devices  11.3 us (30%)
  Pallas kernels  7.32 us (20%)
  other arithmetic  2.84 us (8%)
  local copies, waits for them, and re-layouts  1.46 us (4%)
  between operations  1.36 us (4%)
    ppermute x6, waiting for transfers between devices, scatter_sum(): moved.append(lax.ppermute(chunk.astype(jnp.bfloat16), 'param', pairs))  7.62 us
    ppermute x6, starting transfers between devices, scatter_sum(): moved.append(lax.ppermute(chunk.astype(jnp.bfloat16), 'param', pairs))  6.73 us
    ppermute x2, waiting for transfers between devices, exchange(): moved.append(lax.ppermute(own, axis, pairs))  5.13 us
    ppermute x2, starting transfers between devices, exchange(): moved.append(lax.ppermute(own, axis, pairs))  4.54 us
    pallas_call x1, Pallas kernels, products(): pl.pallas_call(product_kernel, in_specs=[pl.BlockSpec(memory_space=pltpu....  3.72 us
    pallas_call x1, Pallas kernels, transform(): pl.pallas_call(transform_kernel, out_shape=jax.ShapeDtypeStruct((rows, pa...  3.61 us
    concatenate x1, other arithmetic, build_table(): return jnp.concatenate([table_high, table_low], axis=0)  0.82 us
    squeeze x1, local copies, waits for them, and re-layouts, scatter_sum(): lax.dynamic_index_in_dim(terms, (member + step) % count, 0, keepdims=False)  0.8 us
  transfers between devices with their start and end apart: 8, of which 7 were waited for; matrix products, arithmetic and copies ran while one was open for 0% of the time, Pallas kernels for 0%

profile of v1, /device:TPU:0, one launch (start us, length us, event | category | flops | bytes accessed | tf_op | source)
XLA Modules:
  0.0 37.1 jit_solution(17633790795874029948)
XLA Ops:
  1.3 0.5 %fusion.6 = (f32[8,3360]{1,0:T(8,128)S(1)}, f32[8,3360]{1,0:T(8,128)S(1)}) fusion(s32[3360]{0:T(1024)S(1)} %add_select_fusion.1, s32[8]{0:T(128)S(1)} %iota_add_fusion), kind=kLoop, calls=%fused_computation.13 | loop fusion | flops 268800 | bytes 228512 | tf_op jit(solution)/shard_map/cos | solution.py:19
  1.9 0.8 %pad_maximum_fusion.table_ref = f32[32,3360]{1,0:T(8,128)} fusion(f32[16,3360]{1,0:T(8,128)S(1)} %fusion.3, f32[16,3360]{1,0:T(8,128)S(1)} %convert_element_type.92), kind=kLoop, calls=%fused_computation.1 | loop fusion | flops 107520 | bytes 860160 | tf_op jit(solution)/shard_map/concatenate | solution.py:22
  2.8 3.6 %transform.1.refs_0_ = bf16[128,320]{1,0:T(8,128)(2,1)} custom-call(f32[32,3360]{1,0:T(8,128)} %pad_maximum_fusion.table_ref, bf16[3360,320]{1,0:T(8,128)(2,1)} %bitcast.38), custom_call_target="tpu_custom_call" | custom-call | tf_op jit(solution)/shard_map/transform/pallas_call | solution.py:50
  6.4 0.0 copy-start.2
  6.4 3.0 %collective-permute-start = (bf16[128,320]{1,0:T(8,128)(2,1)}, bf16[128,320]{1,0:T(8,128)(2,1)S(1)}, u32[]{:S(2)}, u32[]{:S(2)}) collective-permute-start(bf16[128,320]{1,0:T(8,128)(2,1)} %transform.1.refs_0_), channel_id=1, source_target_pairs={{0,1},{1,0},{2,3},{3,2},{4,5},{5,4},{6,7},{7,6},{8,9},{9,8},{10,11... | collective-permute-start | bytes 245768 | tf_op jit(solution)/shard_map/ppermute | solution.py:102
  9.4 3.0 %collective-permute-done.refs_1_ = bf16[128,320]{1,0:T(8,128)(2,1)S(1)} collective-permute-done((bf16[128,320]{1,0:T(8,128)(2,1)}, bf16[128,320]{1,0:T(8,128)(2,1)S(1)}, u32[]{:S(2)}, u32[]{:S(2)}) %collective-permute-start) | collective-permute-done | bytes 81952 | tf_op jit(solution)/shard_map/ppermute | solution.py:102
  12.4 0.0 copy-start
  12.4 0.6 %copy-done = bf16[128,320]{1,0:T(8,128)(2,1)} copy-done((bf16[128,320]{1,0:T(8,128)(2,1)}, bf16[128,320]{1,0:T(8,128)(2,1)S(1)}, u32[]{:S(2)}) %copy-start) | copy-done | bytes 81944
  13.0 3.7 %products.1 = bf16[16,2,8,256]{3,2,1,0:T(8,128)(2,1)} custom-call(s32[1]{0:T(128)} %bitcast.place_ref, bf16[8,320,2,256]{3,2,1,0:T(2,128)(2,1)} %weights_ref.1, bf16[128,320]{1,0:T(8,128)(2,1)} %transform.1.refs_0_, bf16[128,320]{1,0:T(8,128)(2,1)} %copy-done), custom_call_target="tpu_custom_call" | custom-call | tf_op jit(solution)/shard_map/products/pallas_call | solution.py:112
  16.7 0.8 %dynamic-slice_bitcast_fusion.2 = (bf16[4,1,2,8,256]{4,3,2,1,0:T(8,128)(2,1)S(1)}, bf16[4,1,2,8,256]{4,3,2,1,0:T(8,128)(2,1)S(1)}, bf16[4,1,2,8,256]{4,3,2,1,0:T(8,128)(2,1)S(1)}) fusion(bf16[4,4,1,2,8,256]{5,4,3,1,0,2:T(8,128)(2,1)} %bitcast.39, s32[]{:T(128)S(6)} %select_n.87, s32[]{:T(128)S(6)} %select_n.89, s32[]{:T(128)S(6)} %select_n.91), kind=kLoop, calls=%fused_computation.20 | loop fusion | bytes 196620 | tf_op jit(solution)/shard_map/jit(dynamic_index_in_dim)/squeeze | solution.py:134
  17.5 3.9 %collective-permute-start.3 = (bf16[4,1,2,8,256]{4,3,2,1,0:T(8,128)(2,1)S(1)}, bf16[4,1,2,8,256]{4,3,2,1,0:T(8,128)(2,1)S(1)}, u32[]{:S(2)}, u32[]{:S(2)}) collective-permute-start(bf16[4,1,2,8,256]{4,3,2,1,0:T(8,128)(2,1)S(1)} %get-tuple-element.4), channel_id=1, source_target_pairs={{0,24},{2,26},{4,28},{6,30},{8,0},{10,2},{12,4},{14,6},{16,8},{18,... | collective-permute-start | bytes 98312 | tf_op jit(solution)/shard_map/ppermute | solution.py:135
  21.5 0.0 collective-permute-start.2
  21.5 1.0 %collective-permute-start.1 = (bf16[4,1,2,8,256]{4,3,2,1,0:T(8,128)(2,1)S(1)}, bf16[4,1,2,8,256]{4,3,2,1,0:T(8,128)(2,1)S(1)}, u32[]{:S(2)}, u32[]{:S(2)}) collective-permute-start(bf16[4,1,2,8,256]{4,3,2,1,0:T(8,128)(2,1)S(1)} %get-tuple-element.2), channel_id=1, source_target_pairs={{0,8},{2,10},{4,12},{6,14},{8,16},{10,18},{12,20},{14,22},{16,24},... | collective-permute-start | bytes 98312 | tf_op jit(solution)/shard_map/ppermute | solution.py:135
  22.5 0.6 %collective-permute-done.3 = bf16[4,1,2,8,256]{4,3,2,1,0:T(8,128)(2,1)S(1)} collective-permute-done((bf16[4,1,2,8,256]{4,3,2,1,0:T(8,128)(2,1)S(1)}, bf16[4,1,2,8,256]{4,3,2,1,0:T(8,128)(2,1)S(1)}, u32[]{:S(2)}, u32[]{:S(2)}) %collective-permute-start.3) | collective-permute-done | bytes 32800 | tf_op jit(solution)/shard_map/ppermute | solution.py:135
  23.1 3.2 %collective-permute-done.2 = bf16[4,1,2,8,256]{4,3,2,1,0:T(8,128)(2,1)S(1)} collective-permute-done((bf16[4,1,2,8,256]{4,3,2,1,0:T(8,128)(2,1)S(1)}, bf16[4,1,2,8,256]{4,3,2,1,0:T(8,128)(2,1)S(1)}, u32[]{:S(2)}, u32[]{:S(2)}) %collective-permute-start.2) | collective-permute-done | bytes 32800 | tf_op jit(solution)/shard_map/ppermute | solution.py:135
  26.3 0.9 %collective-permute-done.1 = bf16[4,1,2,8,256]{4,3,2,1,0:T(8,128)(2,1)S(1)} collective-permute-done((bf16[4,1,2,8,256]{4,3,2,1,0:T(8,128)(2,1)S(1)}, bf16[4,1,2,8,256]{4,3,2,1,0:T(8,128)(2,1)S(1)}, u32[]{:S(2)}, u32[]{:S(2)}) %collective-permute-start.1) | collective-permute-done | bytes 32800 | tf_op jit(solution)/shard_map/ppermute | solution.py:135
  27.2 0.8 %fusion.9 = f32[4,1,2,8,256]{4,3,2,1,0:T(8,128)S(1)} fusion(bf16[4,1,2,8,256]{4,3,2,1,0:T(8,128)(2,1)S(1)} %collective-permute-done.3, bf16[4,1,2,8,256]{4,3,2,1,0:T(8,128)(2,1)S(1)} %collective-permute-done.2, bf16[4,1,2,8,256]{4,3,2,1,0:T(8,128)(2,1)S(1)} %collective-permute-done.1, bf16[4,4,1,2,8,256]{5,4,3,1,2,0:T(8,128)(2,1)} %bitcast.40, s32[]{:T(128)S(6)} %select_n.85), kind=kLoop, calls=%fused_computation.17 | loop fusion | flops 114688 | bytes 196612 | tf_op jit(solution)/shard_map/add | solution.py:138
  28.0 0.1 collective-permute-start.6
  28.0 1.6 %collective-permute-start.5 = (bf16[1,2,8,256]{3,2,1,0:T(8,128)(2,1)S(1)}, bf16[1,2,8,256]{3,2,1,0:T(8,128)(2,1)S(1)}, u32[]{:S(2)}, u32[]{:S(2)}) collective-permute-start(bf16[1,2,8,256]{3,2,1,0:T(8,128)(2,1)S(1)} %get-tuple-element.7), channel_id=1, source_target_pairs={{0,4},{2,6},{4,0},{6,2},{8,12},{10,14},{12,8},{14,10},{16,20},{18,... | collective-permute-start | bytes 24584 | tf_op jit(solution)/shard_map/ppermute | solution.py:135
  29.6 0.2 collective-permute-start.4
  29.8 0.0 collective-permute-done.6
  29.8 2.0 %collective-permute-done.5 = bf16[1,2,8,256]{3,2,1,0:T(8,128)(2,1)S(1)} collective-permute-done((bf16[1,2,8,256]{3,2,1,0:T(8,128)(2,1)S(1)}, bf16[1,2,8,256]{3,2,1,0:T(8,128)(2,1)S(1)}, u32[]{:S(2)}, u32[]{:S(2)}) %collective-permute-start.5) | collective-permute-done | bytes 8224 | tf_op jit(solution)/shard_map/ppermute | solution.py:135
  31.8 0.9 %collective-permute-done.4 = bf16[1,2,8,256]{3,2,1,0:T(8,128)(2,1)S(1)} collective-permute-done((bf16[1,2,8,256]{3,2,1,0:T(8,128)(2,1)S(1)}, bf16[1,2,8,256]{3,2,1,0:T(8,128)(2,1)S(1)}, u32[]{:S(2)}, u32[]{:S(2)}) %collective-permute-start.4) | collective-permute-done | bytes 8224 | tf_op jit(solution)/shard_map/ppermute | solution.py:135
  32.7 0.0 copy-done.2
  32.7 0.0 copy-start.1
  32.7 0.1 convolution_bitcast_fusion
  32.8 1.5 %collective-permute-start.7 = (f32[1,2,8,16]{3,2,1,0:T(8,128)S(1)}, f32[1,2,8,16]{3,2,1,0:T(8,128)S(1)}, u32[]{:S(2)}, u32[]{:S(2)}) collective-permute-start(f32[1,2,8,16]{3,2,1,0:T(8,128)S(1)} %convolution_bitcast_fusion), channel_id=1, source_target_pairs={{0,1},{1,0},{2,3},{3,2},{4,5},{5,4},{6,7},{7,6},{8,9},{9,8},{10,11... | collective-permute-start | bytes 3080 | tf_op jit(solution)/shard_map/ppermute | solution.py:102
  34.4 2.1 %collective-permute-done.7 = f32[1,2,8,16]{3,2,1,0:T(8,128)S(1)} collective-permute-done((f32[1,2,8,16]{3,2,1,0:T(8,128)S(1)}, f32[1,2,8,16]{3,2,1,0:T(8,128)S(1)}, u32[]{:S(2)}, u32[]{:S(2)}) %collective-permute-start.7) | collective-permute-done | bytes 1056 | tf_op jit(solution)/shard_map/ppermute | solution.py:102
  36.5 0.6 %add_multiply_fusion = f32[1,2,8,16]{3,2,1,0:T(8,128)} fusion(f32[1,2,8,16]{3,2,1,0:T(8,128)S(1)} %convolution_bitcast_fusion, f32[1,2,8,16]{3,2,1,0:T(8,128)S(1)} %collective-permute-done.7), kind=kLoop, calls=%fused_computation.40 | loop fusion | flops 512 | bytes 3072 | tf_op jit(solution)/shard_map/mul | solution.py:165
  37.1 0.0 copy-done.1
  (7 shorter events, 0.1 us)
Async XLA Ops:
  6.4 26.3 %copy-start.2 = (s32[256]{0:T(256)S(1)}, s32[256]{0:T(256)}, u32[]{:S(2)}) copy-start(s32[256]{0:T(256)} %param.7) | copy-start | bytes 3076
  6.4 6.0 %collective-permute-start = (bf16[128,320]{1,0:T(8,128)(2,1)}, bf16[128,320]{1,0:T(8,128)(2,1)S(1)}, u32[]{:S(2)}, u32[]{:S(2)}) collective-permute-start(bf16[128,320]{1,0:T(8,128)(2,1)} %transform.1.refs_0_), channel_id=1, source_target_pairs={{0,1},{1,0},{2,3},{3,2},{4,5},{5,4},{6,7},{7,6},{8,9},{9,8},{10,11... | collective-permute-start | bytes 245768 | tf_op jit(solution)/shard_map/ppermute | solution.py:102
  12.4 0.6 %copy-start = (bf16[128,320]{1,0:T(8,128)(2,1)}, bf16[128,320]{1,0:T(8,128)(2,1)S(1)}, u32[]{:S(2)}) copy-start(bf16[128,320]{1,0:T(8,128)(2,1)S(1)} %collective-permute-done.refs_1_) | copy-start | bytes 245764
  17.5 5.5 %collective-permute-start.3 = (bf16[4,1,2,8,256]{4,3,2,1,0:T(8,128)(2,1)S(1)}, bf16[4,1,2,8,256]{4,3,2,1,0:T(8,128)(2,1)S(1)}, u32[]{:S(2)}, u32[]{:S(2)}) collective-permute-start(bf16[4,1,2,8,256]{4,3,2,1,0:T(8,128)(2,1)S(1)} %get-tuple-element.4), channel_id=1, source_target_pairs={{0,24},{2,26},{4,28},{6,30},{8,0},{10,2},{12,4},{14,6},{16,8},{18,... | collective-permute-start | bytes 98312 | tf_op jit(solution)/shard_map/ppermute | solution.py:135
  21.5 4.8 %collective-permute-start.2 = (bf16[4,1,2,8,256]{4,3,2,1,0:T(8,128)(2,1)S(1)}, bf16[4,1,2,8,256]{4,3,2,1,0:T(8,128)(2,1)S(1)}, u32[]{:S(2)}, u32[]{:S(2)}) collective-permute-start(bf16[4,1,2,8,256]{4,3,2,1,0:T(8,128)(2,1)S(1)} %get-tuple-element.3), channel_id=1, source_target_pairs={{0,16},{2,18},{4,20},{6,22},{8,24},{10,26},{12,28},{14,30},{16,0},... | collective-permute-start | bytes 98312 | tf_op jit(solution)/shard_map/ppermute | solution.py:135
  21.5 5.7 %collective-permute-start.1 = (bf16[4,1,2,8,256]{4,3,2,1,0:T(8,128)(2,1)S(1)}, bf16[4,1,2,8,256]{4,3,2,1,0:T(8,128)(2,1)S(1)}, u32[]{:S(2)}, u32[]{:S(2)}) collective-permute-start(bf16[4,1,2,8,256]{4,3,2,1,0:T(8,128)(2,1)S(1)} %get-tuple-element.2), channel_id=1, source_target_pairs={{0,8},{2,10},{4,12},{6,14},{8,16},{10,18},{12,20},{14,22},{16,24},... | collective-permute-start | bytes 98312 | tf_op jit(solution)/shard_map/ppermute | solution.py:135
  28.0 1.8 %collective-permute-start.6 = (bf16[1,2,8,256]{3,2,1,0:T(8,128)(2,1)S(1)}, bf16[1,2,8,256]{3,2,1,0:T(8,128)(2,1)S(1)}, u32[]{:S(2)}, u32[]{:S(2)}) collective-permute-start(bf16[1,2,8,256]{3,2,1,0:T(8,128)(2,1)S(1)} %get-tuple-element.6), channel_id=1, source_target_pairs={{0,6},{2,0},{4,2},{6,4},{8,14},{10,8},{12,10},{14,12},{16,22},{18,... | collective-permute-start | bytes 24584 | tf_op jit(solution)/shard_map/ppermute | solution.py:135
  28.0 3.7 %collective-permute-start.5 = (bf16[1,2,8,256]{3,2,1,0:T(8,128)(2,1)S(1)}, bf16[1,2,8,256]{3,2,1,0:T(8,128)(2,1)S(1)}, u32[]{:S(2)}, u32[]{:S(2)}) collective-permute-start(bf16[1,2,8,256]{3,2,1,0:T(8,128)(2,1)S(1)} %get-tuple-element.7), channel_id=1, source_target_pairs={{0,4},{2,6},{4,0},{6,2},{8,12},{10,14},{12,8},{14,10},{16,20},{18,... | collective-permute-start | bytes 24584 | tf_op jit(solution)/shard_map/ppermute | solution.py:135
  29.6 3.1 %collective-permute-start.4 = (bf16[1,2,8,256]{3,2,1,0:T(8,128)(2,1)S(1)}, bf16[1,2,8,256]{3,2,1,0:T(8,128)(2,1)S(1)}, u32[]{:S(2)}, u32[]{:S(2)}) collective-permute-start(bf16[1,2,8,256]{3,2,1,0:T(8,128)(2,1)S(1)} %get-tuple-element.5), channel_id=1, source_target_pairs={{0,2},{2,4},{4,6},{6,0},{8,10},{10,12},{12,14},{14,8},{16,18},{18,... | collective-permute-start | bytes 24584 | tf_op jit(solution)/shard_map/ppermute | solution.py:135
  32.7 4.4 %copy-start.1 = (f32[1,2,8,256]{3,2,1,0:T(8,128)}, f32[1,2,8,256]{3,2,1,0:T(8,128)S(1)}, u32[]{:S(2)}) copy-start(f32[1,2,8,256]{3,2,1,0:T(8,128)S(1)} %fusion.14) | copy-start | bytes 49156
  32.8 3.7 %collective-permute-start.7 = (f32[1,2,8,16]{3,2,1,0:T(8,128)S(1)}, f32[1,2,8,16]{3,2,1,0:T(8,128)S(1)}, u32[]{:S(2)}, u32[]{:S(2)}) collective-permute-start(f32[1,2,8,16]{3,2,1,0:T(8,128)S(1)} %convolution_bitcast_fusion), channel_id=1, source_target_pairs={{0,1},{1,0},{2,3},{3,2},{4,5},{5,4},{6,7},{7,6},{8,9},{9,8},{10,11... | collective-permute-start | bytes 3080 | tf_op jit(solution)/shard_map/ppermute | solution.py:102

commit v2 on v1

v2 whole, which is shorter than its diff:
```python
import math

import jax
import jax.numpy as jnp
from jax import lax
from jax.experimental import pallas as pl
from jax.experimental.pallas import tpu as pltpu
from jax.sharding import PartitionSpec as P

GROUPS = 16
SCOPED = 24 << 20
SINE = (-1 / 6, 1 / 120, -1 / 5040, 1 / 362880, -1 / 39916800, 1 / 6227020800)


def quarter_sine(turns):
    angle = turns * (2.0 * math.pi)
    square = angle * angle
    series = jnp.full_like(square, SINE[-1])
    for term in SINE[-2::-1]:
        series = series * square + term
    return angle + angle * square * series


def transform_kernel(start_ref, series_ref, spectrum_ref, table_ref, spread_ref, held_ref, sem):
    table_rows, columns = table_ref.shape
    freq_count = table_rows // 4
    series_count = spread_ref.shape[0] // table_rows
    steps_count = columns // series_count
    copy = pltpu.make_async_copy(series_ref, held_ref, sem)
    copy.start()
    table_shape = (freq_count, columns)
    step = (lax.broadcasted_iota(jnp.int32, table_shape, 1) // series_count).astype(jnp.float32)
    freq = (start_ref[0] + lax.broadcasted_iota(jnp.int32, table_shape, 0)).astype(jnp.float32)
    phase = step * freq
    phase = phase - jnp.floor(phase * (1.0 / steps_count) + 0.5) * steps_count
    near = jnp.where(phase > steps_count / 4, steps_count / 2 - phase, phase)
    near = jnp.where(phase < -steps_count / 4, -steps_count / 2 - phase, near)
    scale = 1.0 / math.sqrt(steps_count)
    cosine = quarter_sine((steps_count / 4 - jnp.abs(phase)) / steps_count) * scale
    sine = quarter_sine(near / steps_count) * -scale
    for kind, value in enumerate((cosine, sine)):
        high = value.astype(jnp.bfloat16).astype(jnp.float32)
        table_ref[kind * freq_count : (kind + 1) * freq_count, :] = high
        table_ref[(kind + 2) * freq_count : (kind + 3) * freq_count, :] = value - high
    shape = (series_count, columns)
    own = lax.broadcasted_iota(jnp.int32, shape, 1) % series_count == lax.broadcasted_iota(
        jnp.int32, shape, 0
    )
    for row in range(0, table_rows, 2):
        pair = [
            jnp.where(own, jnp.broadcast_to(table_ref[one : one + 1, :], shape), 0.0)
            for one in (row, row + 1)
        ]
        spread_ref[row * series_count : (row + 2) * series_count, :] = jnp.concatenate(
            pair, axis=0
        ).astype(jnp.bfloat16)
    copy.wait()
    halves = jnp.dot(spread_ref[...], held_ref[...], preferred_element_type=jnp.float32)
    half = halves.shape[0] // 2
    spectrum_ref[...] = (halves[:half] + halves[half:]).astype(jnp.bfloat16)


def transform(samples, block_start, freq_count):
    series_count, param_local, steps_count = samples.shape
    series = samples.transpose(2, 0, 1).reshape(steps_count * series_count, param_local)
    rows = 2 * freq_count * series_count
    return pl.pallas_call(
        transform_kernel,
        in_specs=[pl.BlockSpec(memory_space=pltpu.SMEM), pl.BlockSpec(memory_space=pl.ANY)],
        out_shape=pltpu.VMEM((rows, param_local), jnp.bfloat16),
        scratch_shapes=[
            pltpu.VMEM((4 * freq_count, steps_count * series_count), jnp.float32),
            pltpu.VMEM((2 * rows, steps_count * series_count), jnp.bfloat16),
            pltpu.VMEM(series.shape, series.dtype),
            pltpu.SemaphoreType.DMA,
        ],
        compiler_params=pltpu.CompilerParams(vmem_limit_bytes=SCOPED),
        name="transform",
    )(block_start, series)


def product_of(spectrum_ref, weights_ref, stage_ref):
    freq_count, param_local, _, gauge_local = weights_ref.shape
    series_count = spectrum_ref.shape[0] // (2 * freq_count)
    shape = (param_local, 2 * param_local)
    double = (
        lax.broadcasted_iota(jnp.int32, shape, 1) // 2 == lax.broadcasted_iota(jnp.int32, shape, 0)
    )
    double = jnp.where(double, 1.0, 0.0).astype(jnp.bfloat16)
    spread = jnp.dot(spectrum_ref[...], double, preferred_element_type=jnp.float32)
    even = lax.broadcasted_iota(jnp.int32, (series_count, 2 * param_local), 1) % 2 == 0
    for freq in range(freq_count):
        real, imag = [
            spread[(kind * freq_count + freq) * series_count :][:series_count] for kind in (0, 1)
        ]
        rows = jnp.concatenate(
            [jnp.where(even, real, -imag), jnp.where(even, imag, real)], axis=0
        ).astype(jnp.bfloat16)
        weights = weights_ref[freq].reshape(2 * param_local, gauge_local)
        product = jnp.dot(rows, weights, preferred_element_type=jnp.float32)
        stage_ref[:, 0, freq, :] = product[:series_count]
        stage_ref[:, 1, freq, :] = product[series_count:]
    return stage_ref[...].astype(jnp.bfloat16)


def own_kernel(weights_ref, spectrum_ref, terms_ref, stage_ref):
    terms_ref[...] = product_of(spectrum_ref, weights_ref, stage_ref)


def other_kernel(place_ref, weights_ref, own_ref, *refs):
    *spectra_refs, terms_ref, stage_ref = refs
    parts = len(spectra_refs) + 1
    terms_ref[place_ref[0]] = own_ref[...]
    for step, ref in enumerate(spectra_refs):
        terms_ref[lax.rem(place_ref[0] + step + 1, parts)] = product_of(ref, weights_ref, stage_ref)


def exchange(own, axis):
    count = lax.axis_size(axis)
    moved = [own]
    for step in range(1, count):
        pairs = [(source, (source - step) % count) for source in range(count)]
        moved.append(lax.ppermute(own, axis, pairs))
    return moved


def in_fast(value):
    return pltpu.with_memory_space_constraint(value, pltpu.VMEM)


def products(spectrum, operator_rows):
    freq_count, param_local, _, gauge_local = operator_rows.shape
    weights = in_fast(operator_rows)
    spectra = [in_fast(one) for one in exchange(spectrum, "qoi")]
    place = lax.axis_index("qoi").astype(jnp.int32).reshape(1)
    series_count = spectrum.shape[0] // (2 * freq_count)
    shape = (series_count, 2, freq_count, gauge_local)
    work = 8 * series_count * param_local * freq_count * gauge_local
    in_vmem = pl.BlockSpec(memory_space=pltpu.VMEM)
    own = pl.pallas_call(
        own_kernel,
        in_specs=[in_vmem] * 2,
        out_shape=pltpu.VMEM(shape, jnp.bfloat16),
        scratch_shapes=[pltpu.VMEM(shape, jnp.float32)],
        cost_estimate=pl.CostEstimate(flops=8 * work, bytes_accessed=weights.size, transcendentals=0),
        compiler_params=pltpu.CompilerParams(vmem_limit_bytes=SCOPED),
        name="own_products",
    )(weights, spectra[0])
    if len(spectra) == 1:
        return own
    terms = pl.pallas_call(
        other_kernel,
        in_specs=[pl.BlockSpec(memory_space=pltpu.SMEM)] + [in_vmem] * (1 + len(spectra)),
        out_shape=pltpu.VMEM((len(spectra),) + shape, jnp.bfloat16),
        scratch_shapes=[pltpu.VMEM(shape, jnp.float32)],
        compiler_params=pltpu.CompilerParams(vmem_limit_bytes=SCOPED),
        name="other_products",
    )(place, weights, in_fast(own), *spectra[1:])
    return terms.reshape((len(spectra) * series_count,) + shape[1:])


def scatter_sum(terms, stride, count):
    total = lax.axis_size("param")
    member = lax.axis_index("param") // stride % count
    moved = []
    for step in range(1, count):
        pairs = []
        for source in range(total):
            place = source // stride % count
            pairs.append((source, source + ((place + step) % count - place) * stride))
        chunk = lax.dynamic_index_in_dim(terms, (member + step) % count, 0, keepdims=False)
        moved.append(lax.ppermute(chunk.astype(jnp.bfloat16), "param", pairs))
    result = lax.dynamic_index_in_dim(terms, member, 0, keepdims=False).astype(jnp.float32)
    for one in moved:
        result = result + one.astype(jnp.float32)
    return result


def local(samples, operator_rows, block_start, gauge_group):
    freq_count = operator_rows.shape[0]
    gauge_local = operator_rows.shape[3]
    terms = products(transform(samples, block_start, freq_count), operator_rows)
    param_count = lax.axis_size("param")
    own_rows = terms.shape[0] // param_count
    inner = 4 if param_count % 4 == 0 else 1
    outer = param_count // inner
    rest = (own_rows, 2, freq_count, gauge_local)
    half_sums = scatter_sum(terms.reshape((outer, inner) + rest), inner, outer)
    qoi_spectrum = scatter_sum(half_sums, 1, inner)
    onehot = (gauge_group[:, None] == jnp.arange(GROUPS, dtype=jnp.int32)[None, :]).astype(
        jnp.float32
    )
    local_sums = jnp.dot(
        qoi_spectrum.reshape(-1, gauge_local),
        onehot,
        precision=lax.Precision.HIGHEST,
        preferred_element_type=jnp.float32,
    )
    local_sums = local_sums.reshape(own_rows, 2, freq_count, GROUPS)
    summed = sum(exchange(local_sums, "qoi"))
    norm_factor = math.sqrt(GROUPS / (gauge_local * lax.axis_size("qoi")))
    return (qoi_spectrum, summed * norm_factor)


def solution(mesh):
    return jax.shard_map(
        local,
        mesh=mesh,
        in_specs=(P("qoi", "param", None), P(None, "param", None, "qoi"), P(), P("qoi")),
        out_specs=(P("param", None, None, "qoi"), P("param", None, None, None)),
        check_vma=False,
    )
```

time: 37.5 us -> 31.3 us (0.83)
  Pallas kernels: 7.32 us -> 4.26 us
  other arithmetic: 2.84 us -> 0.63 us
  waiting for transfers between devices: 12.7 us -> 11.5 us
    pallas_call x2 -> x3, Pallas kernels: 7.32 us -> 4.26 us  [the longest x1 2.18 us: transform(): pl.pallas_call(transform_kernel, in_specs=[pl.BlockSpec(memory_space=pltp...]
    ppermute x2, waiting for transfers between devices: 5.13 us -> 3.88 us  [exchange(): moved.append(lax.ppermute(own, axis, pairs))]
    unnamed x6 -> x8, local copies, waits for them, and re-layouts: 0.65 us -> 1.74 us
    concatenate x1 -> x0, other arithmetic: 0.82 us -> none  [build_table(): return jnp.concatenate([table_high, table_low], axis=0)]
    squeeze x1, local copies, waits for them, and re-layouts: 0.8 us -> 0.02 us  [scatter_sum(): lax.dynamic_index_in_dim(terms, (member + step) % count, 0, keepdims=False)]
    add x2, other arithmetic: 0.78 us -> 0.03 us  [scatter_sum(): result = result + one.astype(jnp.float32)]
    cos x1 -> x0, other arithmetic: 0.55 us -> none  [build_table(): jnp.cos(phases)]
  transfers between devices with their start and end apart: 8 -> 8, of which waited for: 7 -> 7; matrix products, arithmetic and copies ran while one was open for 0% -> 0% of each run, Pallas kernels for 0% -> 3%
where the time goes in v2:
time: 31.3 us; the launch traced here: 31.1 us
  waiting for transfers between devices  11.5 us (37%)
  starting transfers between devices  11.3 us (36%)
  Pallas kernels  4.26 us (14%)
  local copies, waits for them, and re-layouts  1.77 us (6%)
  between operations  1.52 us (5%)
  other arithmetic  0.63 us (2%)
    ppermute x6, waiting for transfers between devices, scatter_sum(): moved.append(lax.ppermute(chunk.astype(jnp.bfloat16), 'param', pairs))  7.62 us
    ppermute x6, starting transfers between devices, scatter_sum(): moved.append(lax.ppermute(chunk.astype(jnp.bfloat16), 'param', pairs))  6.74 us
    ppermute x2, starting transfers between devices, exchange(): moved.append(lax.ppermute(own, axis, pairs))  4.6 us
    ppermute x2, waiting for transfers between devices, exchange(): moved.append(lax.ppermute(own, axis, pairs))  3.88 us
    pallas_call x1, Pallas kernels, transform(): pl.pallas_call(transform_kernel, in_specs=[pl.BlockSpec(memory_space=pltp...  2.18 us
    unnamed x8, local copies, waits for them, and re-layouts  1.74 us
    pallas_call x1, Pallas kernels, products(): pl.pallas_call(other_kernel, in_specs=[pl.BlockSpec(memory_space=pltpu.SM...  1.04 us
    pallas_call x1, Pallas kernels, products(): pl.pallas_call(own_kernel, in_specs=[in_vmem] * 2, out_shape=pltpu.VMEM(s...  1.04 us
  transfers between devices with their start and end apart: 8, of which 7 were waited for; matrix products, arithmetic and copies ran while one was open for 0% of the time, Pallas kernels for 3%

profile of v2, /device:TPU:0, one launch (start us, length us, event | category | flops | bytes accessed | tf_op | source)
XLA Modules:
  0.0 31.1 jit_solution(14794702606366656007)
XLA Ops:
  0.6 0.0 copy-start
  1.4 0.0 copy-start.1
  1.4 1.7 %copy-done.1 = bf16[8,320,420]{1,0,2:T(8,128)(2,1)S(1)} copy-done((bf16[8,320,420]{1,0,2:T(8,128)(2,1)S(1)}, bf16[8,320,420]{1,0,2:T(8,128)(2,1)}, u32[]{:S(2)}) %copy-start.1) | copy-done | bytes 2150424
  3.2 2.2 %transform.1.spectrum_ref = bf16[128,320]{1,0:T(8,128)(2,1)S(1)} custom-call(s32[1]{0:T(128)S(6)} %copy.7.start_ref, bf16[3360,320]{1,0:T(8,128)(2,1)S(1)} %bitcast.36), custom_call_target="tpu_custom_call" | custom-call | tf_op jit(solution)/shard_map/transform/pallas_call | solution.py:67
  5.4 3.1 %collective-permute-start = (bf16[128,320]{1,0:T(8,128)(2,1)S(1)}, bf16[128,320]{1,0:T(8,128)(2,1)S(1)}, u32[]{:S(2)}, u32[]{:S(2)}) collective-permute-start(bf16[128,320]{1,0:T(8,128)(2,1)S(1)} %transform.1.spectrum_ref), channel_id=1, source_target_pairs={{0,1},{1,0},{2,3},{3,2},{4,5},{5,4},{6,7},{7,6},{8,9},{9,8},{10,11... | collective-permute-start | bytes 245768 | tf_op jit(solution)/shard_map/ppermute | solution.py:123
  8.4 0.0 copy-done
  8.4 0.0 copy-start.3
  8.4 1.0 %own_products.1.own_ref = bf16[8,2,8,256]{3,2,1,0:T(8,128)(2,1)S(1)} custom-call(bf16[8,320,2,256]{3,2,1,0:T(2,128)(2,1)S(1)} %copy-done, bf16[128,320]{1,0:T(8,128)(2,1)S(1)} %transform.1.spectrum_ref), custom_call_target="tpu_custom_call" | custom-call | flops 335544320 | bytes 1310720 | tf_op jit(solution)/shard_map/own_products/pallas_call | solution.py:140
  9.5 1.7 %collective-permute-done.refs_0_ = bf16[128,320]{1,0:T(8,128)(2,1)S(1)} collective-permute-done((bf16[128,320]{1,0:T(8,128)(2,1)S(1)}, bf16[128,320]{1,0:T(8,128)(2,1)S(1)}, u32[]{:S(2)}, u32[]{:S(2)}) %collective-permute-start) | collective-permute-done | bytes 81952 | tf_op jit(solution)/shard_map/ppermute | solution.py:123
  11.2 1.0 %other_products.1 = bf16[2,8,2,8,256]{4,3,2,1,0:T(8,128)(2,1)S(1)} custom-call(s32[1]{0:T(128)} %bitcast.place_ref, bf16[8,320,2,256]{3,2,1,0:T(2,128)(2,1)S(1)} %copy-done, bf16[8,2,8,256]{3,2,1,0:T(8,128)(2,1)S(1)} %own_products.1.own_ref, bf16[128,320]{1,0:T(8,128)(2,1)S(1)} %collective-permute-done.refs_0_), custom_call_target="tpu_custom_call" | custom-call | tf_op jit(solution)/shard_map/other_products/pallas_call | solution.py:151
  12.3 4.0 %collective-permute-start.3 = (bf16[4,1,2,8,256]{4,3,2,1,0:T(8,128)(2,1)S(1)}, bf16[4,1,2,8,256]{4,3,2,1,0:T(8,128)(2,1)S(1)}, u32[]{:S(2)}, u32[]{:S(2)}) collective-permute-start(bf16[4,1,2,8,256]{4,3,2,1,0:T(8,128)(2,1)S(1)} %get-tuple-element.4), channel_id=1, source_target_pairs={{0,24},{2,26},{4,28},{6,30},{8,0},{10,2},{12,4},{14,6},{16,8},{18,... | collective-permute-start | bytes 98312 | tf_op jit(solution)/shard_map/ppermute | solution.py:172
  16.2 0.0 collective-permute-start.2
  16.2 1.0 %collective-permute-start.1 = (bf16[4,1,2,8,256]{4,3,2,1,0:T(8,128)(2,1)S(1)}, bf16[4,1,2,8,256]{4,3,2,1,0:T(8,128)(2,1)S(1)}, u32[]{:S(2)}, u32[]{:S(2)}) collective-permute-start(bf16[4,1,2,8,256]{4,3,2,1,0:T(8,128)(2,1)S(1)} %get-tuple-element.2), channel_id=1, source_target_pairs={{0,8},{2,10},{4,12},{6,14},{8,16},{10,18},{12,20},{14,22},{16,24},... | collective-permute-start | bytes 98312 | tf_op jit(solution)/shard_map/ppermute | solution.py:172
  17.3 0.6 %collective-permute-done.3 = bf16[4,1,2,8,256]{4,3,2,1,0:T(8,128)(2,1)S(1)} collective-permute-done((bf16[4,1,2,8,256]{4,3,2,1,0:T(8,128)(2,1)S(1)}, bf16[4,1,2,8,256]{4,3,2,1,0:T(8,128)(2,1)S(1)}, u32[]{:S(2)}, u32[]{:S(2)}) %collective-permute-start.3) | collective-permute-done | bytes 32800 | tf_op jit(solution)/shard_map/ppermute | solution.py:172
  17.8 3.2 %collective-permute-done.2 = bf16[4,1,2,8,256]{4,3,2,1,0:T(8,128)(2,1)S(1)} collective-permute-done((bf16[4,1,2,8,256]{4,3,2,1,0:T(8,128)(2,1)S(1)}, bf16[4,1,2,8,256]{4,3,2,1,0:T(8,128)(2,1)S(1)}, u32[]{:S(2)}, u32[]{:S(2)}) %collective-permute-start.2) | collective-permute-done | bytes 32800 | tf_op jit(solution)/shard_map/ppermute | solution.py:172
  21.1 0.9 %collective-permute-done.1 = bf16[4,1,2,8,256]{4,3,2,1,0:T(8,128)(2,1)S(1)} collective-permute-done((bf16[4,1,2,8,256]{4,3,2,1,0:T(8,128)(2,1)S(1)}, bf16[4,1,2,8,256]{4,3,2,1,0:T(8,128)(2,1)S(1)}, u32[]{:S(2)}, u32[]{:S(2)}) %collective-permute-start.1) | collective-permute-done | bytes 32800 | tf_op jit(solution)/shard_map/ppermute | solution.py:172
  22.0 0.1 collective-permute-start.6
  22.1 1.6 %collective-permute-start.5 = (bf16[1,2,8,256]{3,2,1,0:T(8,128)(2,1)S(1)}, bf16[1,2,8,256]{3,2,1,0:T(8,128)(2,1)S(1)}, u32[]{:S(2)}, u32[]{:S(2)}) collective-permute-start(bf16[1,2,8,256]{3,2,1,0:T(8,128)(2,1)S(1)} %get-tuple-element.7), channel_id=1, source_target_pairs={{0,4},{2,6},{4,0},{6,2},{8,12},{10,14},{12,8},{14,10},{16,20},{18,... | collective-permute-start | bytes 24584 | tf_op jit(solution)/shard_map/ppermute | solution.py:172
  23.6 0.2 collective-permute-start.4
  23.8 0.0 collective-permute-done.6
  23.8 2.0 %collective-permute-done.5 = bf16[1,2,8,256]{3,2,1,0:T(8,128)(2,1)S(1)} collective-permute-done((bf16[1,2,8,256]{3,2,1,0:T(8,128)(2,1)S(1)}, bf16[1,2,8,256]{3,2,1,0:T(8,128)(2,1)S(1)}, u32[]{:S(2)}, u32[]{:S(2)}) %collective-permute-start.5) | collective-permute-done | bytes 8224 | tf_op jit(solution)/shard_map/ppermute | solution.py:172
  25.8 0.9 %collective-permute-done.4 = bf16[1,2,8,256]{3,2,1,0:T(8,128)(2,1)S(1)} collective-permute-done((bf16[1,2,8,256]{3,2,1,0:T(8,128)(2,1)S(1)}, bf16[1,2,8,256]{3,2,1,0:T(8,128)(2,1)S(1)}, u32[]{:S(2)}, u32[]{:S(2)}) %collective-permute-start.4) | collective-permute-done | bytes 8224 | tf_op jit(solution)/shard_map/ppermute | solution.py:172
  26.7 0.0 copy-done.3
  26.7 0.0 copy-start.2
  26.7 0.1 convolution_bitcast_fusion
  26.9 1.5 %collective-permute-start.7 = (f32[1,2,8,16]{3,2,1,0:T(8,128)S(1)}, f32[1,2,8,16]{3,2,1,0:T(8,128)S(1)}, u32[]{:S(2)}, u32[]{:S(2)}) collective-permute-start(f32[1,2,8,16]{3,2,1,0:T(8,128)S(1)} %convolution_bitcast_fusion), channel_id=1, source_target_pairs={{0,1},{1,0},{2,3},{3,2},{4,5},{5,4},{6,7},{7,6},{8,9},{9,8},{10,11... | collective-permute-start | bytes 3080 | tf_op jit(solution)/shard_map/ppermute | solution.py:123
  28.4 2.1 %collective-permute-done.7 = f32[1,2,8,16]{3,2,1,0:T(8,128)S(1)} collective-permute-done((f32[1,2,8,16]{3,2,1,0:T(8,128)S(1)}, f32[1,2,8,16]{3,2,1,0:T(8,128)S(1)}, u32[]{:S(2)}, u32[]{:S(2)}) %collective-permute-start.7) | collective-permute-done | bytes 1056 | tf_op jit(solution)/shard_map/ppermute | solution.py:123
  30.5 0.6 %add_multiply_fusion = f32[1,2,8,16]{3,2,1,0:T(8,128)} fusion(f32[1,2,8,16]{3,2,1,0:T(8,128)S(1)} %convolution_bitcast_fusion, f32[1,2,8,16]{3,2,1,0:T(8,128)S(1)} %collective-permute-done.7), kind=kLoop, calls=%fused_computation.19 | loop fusion | flops 512 | bytes 3072 | tf_op jit(solution)/shard_map/mul | solution.py:202
  31.1 0.0 copy-done.2
  (4 shorter events, 0.1 us)
Async XLA Ops:
  0.6 7.8 %copy-start = (bf16[8,320,2,256]{3,2,1,0:T(2,128)(2,1)S(1)}, bf16[8,320,2,256]{3,2,1,0:T(2,128)(2,1)}, u32[]{:S(2)}) copy-start(bf16[8,320,2,256]{3,2,1,0:T(2,128)(2,1)} %weights_ref.3) | copy-start | bytes 7864324
  1.4 1.7 %copy-start.1 = (bf16[8,320,420]{1,0,2:T(8,128)(2,1)S(1)}, bf16[8,320,420]{1,0,2:T(8,128)(2,1)}, u32[]{:S(2)}) copy-start(bf16[8,320,420]{1,0,2:T(8,128)(2,1)} %param.4) | copy-start | bytes 6451204
  5.4 5.9 %collective-permute-start = (bf16[128,320]{1,0:T(8,128)(2,1)S(1)}, bf16[128,320]{1,0:T(8,128)(2,1)S(1)}, u32[]{:S(2)}, u32[]{:S(2)}) collective-permute-start(bf16[128,320]{1,0:T(8,128)(2,1)S(1)} %transform.1.spectrum_ref), channel_id=1, source_target_pairs={{0,1},{1,0},{2,3},{3,2},{4,5},{5,4},{6,7},{7,6},{8,9},{9,8},{10,11... | collective-permute-start | bytes 245768 | tf_op jit(solution)/shard_map/ppermute | solution.py:123
  8.4 18.3 %copy-start.3 = (s32[256]{0:T(256)S(1)}, s32[256]{0:T(256)}, u32[]{:S(2)}) copy-start(s32[256]{0:T(256)} %param.7) | copy-start | bytes 3076
  12.3 5.6 %collective-permute-start.3 = (bf16[4,1,2,8,256]{4,3,2,1,0:T(8,128)(2,1)S(1)}, bf16[4,1,2,8,256]{4,3,2,1,0:T(8,128)(2,1)S(1)}, u32[]{:S(2)}, u32[]{:S(2)}) collective-permute-start(bf16[4,1,2,8,256]{4,3,2,1,0:T(8,128)(2,1)S(1)} %get-tuple-element.4), channel_id=1, source_target_pairs={{0,24},{2,26},{4,28},{6,30},{8,0},{10,2},{12,4},{14,6},{16,8},{18,... | collective-permute-start | bytes 98312 | tf_op jit(solution)/shard_map/ppermute | solution.py:172
  16.2 4.8 %collective-permute-start.2 = (bf16[4,1,2,8,256]{4,3,2,1,0:T(8,128)(2,1)S(1)}, bf16[4,1,2,8,256]{4,3,2,1,0:T(8,128)(2,1)S(1)}, u32[]{:S(2)}, u32[]{:S(2)}) collective-permute-start(bf16[4,1,2,8,256]{4,3,2,1,0:T(8,128)(2,1)S(1)} %get-tuple-element.3), channel_id=1, source_target_pairs={{0,16},{2,18},{4,20},{6,22},{8,24},{10,26},{12,28},{14,30},{16,0},... | collective-permute-start | bytes 98312 | tf_op jit(solution)/shard_map/ppermute | solution.py:172
  16.2 5.7 %collective-permute-start.1 = (bf16[4,1,2,8,256]{4,3,2,1,0:T(8,128)(2,1)S(1)}, bf16[4,1,2,8,256]{4,3,2,1,0:T(8,128)(2,1)S(1)}, u32[]{:S(2)}, u32[]{:S(2)}) collective-permute-start(bf16[4,1,2,8,256]{4,3,2,1,0:T(8,128)(2,1)S(1)} %get-tuple-element.2), channel_id=1, source_target_pairs={{0,8},{2,10},{4,12},{6,14},{8,16},{10,18},{12,20},{14,22},{16,24},... | collective-permute-start | bytes 98312 | tf_op jit(solution)/shard_map/ppermute | solution.py:172
  22.0 1.8 %collective-permute-start.6 = (bf16[1,2,8,256]{3,2,1,0:T(8,128)(2,1)S(1)}, bf16[1,2,8,256]{3,2,1,0:T(8,128)(2,1)S(1)}, u32[]{:S(2)}, u32[]{:S(2)}) collective-permute-start(bf16[1,2,8,256]{3,2,1,0:T(8,128)(2,1)S(1)} %get-tuple-element.6), channel_id=1, source_target_pairs={{0,6},{2,0},{4,2},{6,4},{8,14},{10,8},{12,10},{14,12},{16,22},{18,... | collective-permute-start | bytes 24584 | tf_op jit(solution)/shard_map/ppermute | solution.py:172
  22.1 3.7 %collective-permute-start.5 = (bf16[1,2,8,256]{3,2,1,0:T(8,128)(2,1)S(1)}, bf16[1,2,8,256]{3,2,1,0:T(8,128)(2,1)S(1)}, u32[]{:S(2)}, u32[]{:S(2)}) collective-permute-start(bf16[1,2,8,256]{3,2,1,0:T(8,128)(2,1)S(1)} %get-tuple-element.7), channel_id=1, source_target_pairs={{0,4},{2,6},{4,0},{6,2},{8,12},{10,14},{12,8},{14,10},{16,20},{18,... | collective-permute-start | bytes 24584 | tf_op jit(solution)/shard_map/ppermute | solution.py:172
  23.6 3.1 %collective-permute-start.4 = (bf16[1,2,8,256]{3,2,1,0:T(8,128)(2,1)S(1)}, bf16[1,2,8,256]{3,2,1,0:T(8,128)(2,1)S(1)}, u32[]{:S(2)}, u32[]{:S(2)}) collective-permute-start(bf16[1,2,8,256]{3,2,1,0:T(8,128)(2,1)S(1)} %get-tuple-element.5), channel_id=1, source_target_pairs={{0,2},{2,4},{4,6},{6,0},{8,10},{10,12},{12,14},{14,8},{16,18},{18,... | collective-permute-start | bytes 24584 | tf_op jit(solution)/shard_map/ppermute | solution.py:172
  26.7 4.4 %copy-start.2 = (f32[1,2,8,256]{3,2,1,0:T(8,128)}, f32[1,2,8,256]{3,2,1,0:T(8,128)S(1)}, u32[]{:S(2)}) copy-start(f32[1,2,8,256]{3,2,1,0:T(8,128)S(1)} %fusion.4) | copy-start | bytes 49156
  26.9 3.7 %collective-permute-start.7 = (f32[1,2,8,16]{3,2,1,0:T(8,128)S(1)}, f32[1,2,8,16]{3,2,1,0:T(8,128)S(1)}, u32[]{:S(2)}, u32[]{:S(2)}) collective-permute-start(f32[1,2,8,16]{3,2,1,0:T(8,128)S(1)} %convolution_bitcast_fusion), channel_id=1, source_target_pairs={{0,1},{1,0},{2,3},{3,2},{4,5},{5,4},{6,7},{7,6},{8,9},{9,8},{10,11... | collective-permute-start | bytes 3080 | tf_op jit(solution)/shard_map/ppermute | solution.py:123

commit v3 on v2

--- a/solution.py
+++ b/solution.py
@@ -21,7 +21,9 @@
     return angle + angle * square * series
 
 
-def transform_kernel(start_ref, series_ref, spectrum_ref, table_ref, spread_ref, held_ref, sem):
+def transform_kernel(
+    start_ref, series_ref, spectrum_ref, table_ref, spread_ref, held_ref, sem
+):
     table_rows, columns = table_ref.shape
     freq_count = table_rows // 4
     series_count = spread_ref.shape[0] // table_rows
@@ -63,10 +65,11 @@
 def transform(samples, block_start, freq_count):
     series_count, param_local, steps_count = samples.shape
     series = samples.transpose(2, 0, 1).reshape(steps_count * series_count, param_local)
+    series = pltpu.with_memory_space_constraint(series, pltpu.HBM)
     rows = 2 * freq_count * series_count
     return pl.pallas_call(
         transform_kernel,
-        in_specs=[pl.BlockSpec(memory_space=pltpu.SMEM), pl.BlockSpec(memory_space=pl.ANY)],
+        in_specs=[pl.BlockSpec(memory_space=pltpu.SMEM), pl.BlockSpec(memory_space=pltpu.HBM)],
         out_shape=pltpu.VMEM((rows, param_local), jnp.bfloat16),
         scratch_shapes=[
             pltpu.VMEM((4 * freq_count, steps_count * series_count), jnp.float32),
@@ -79,7 +82,7 @@
     )(block_start, series)
 
 
-def product_of(spectrum_ref, weights_ref, stage_ref):
+def product_of(spectrum_ref, weights_ref, stage_ref, copies=()):
     freq_count, param_local, _, gauge_local = weights_ref.shape
     series_count = spectrum_ref.shape[0] // (2 * freq_count)
     shape = (param_local, 2 * param_local)
@@ -96,6 +99,8 @@
         rows = jnp.concatenate(
             [jnp.where(even, real, -imag), jnp.where(even, imag, real)], axis=0
         ).astype(jnp.bfloat16)
+        if copies:
+            copies[freq].wait()
         weights = weights_ref[freq].reshape(2 * param_local, gauge_local)
         product = jnp.dot(rows, weights, preferred_element_type=jnp.float32)
         stage_ref[:, 0, freq, :] = product[:series_count]
@@ -103,8 +108,14 @@
     return stage_ref[...].astype(jnp.bfloat16)
 
 
-def own_kernel(weights_ref, spectrum_ref, terms_ref, stage_ref):
-    terms_ref[...] = product_of(spectrum_ref, weights_ref, stage_ref)
+def own_kernel(weights_ref, spectrum_ref, terms_ref, held_ref, stage_ref, sems):
+    copies = [
+        pltpu.make_async_copy(weights_ref.at[freq], held_ref.at[freq], sems.at[freq])
+        for freq in range(weights_ref.shape[0])
+    ]
+    for copy in copies:
+        copy.start()
+    terms_ref[...] = product_of(spectrum_ref, held_ref, stage_ref, copies)
 
 
 def other_kernel(place_ref, weights_ref, own_ref, *refs):
@@ -130,22 +141,24 @@
 
 def products(spectrum, operator_rows):
     freq_count, param_local, _, gauge_local = operator_rows.shape
-    weights = in_fast(operator_rows)
     spectra = [in_fast(one) for one in exchange(spectrum, "qoi")]
     place = lax.axis_index("qoi").astype(jnp.int32).reshape(1)
     series_count = spectrum.shape[0] // (2 * freq_count)
     shape = (series_count, 2, freq_count, gauge_local)
     work = 8 * series_count * param_local * freq_count * gauge_local
     in_vmem = pl.BlockSpec(memory_space=pltpu.VMEM)
-    own = pl.pallas_call(
+    own, weights = pl.pallas_call(
         own_kernel,
-        in_specs=[in_vmem] * 2,
-        out_shape=pltpu.VMEM(shape, jnp.bfloat16),
-        scratch_shapes=[pltpu.VMEM(shape, jnp.float32)],
-        cost_estimate=pl.CostEstimate(flops=8 * work, bytes_accessed=weights.size, transcendentals=0),
+        in_specs=[pl.BlockSpec(memory_space=pl.ANY), in_vmem],
+        out_shape=(
+            pltpu.VMEM(shape, jnp.bfloat16),
+            pltpu.VMEM(operator_rows.shape, operator_rows.dtype),
+        ),
+        scratch_shapes=[pltpu.VMEM(shape, jnp.float32), pltpu.SemaphoreType.DMA((freq_count,))],
+        cost_estimate=pl.CostEstimate(flops=8 * work, bytes_accessed=operator_rows.size, transcendentals=0),
         compiler_params=pltpu.CompilerParams(vmem_limit_bytes=SCOPED),
         name="own_products",
-    )(weights, spectra[0])
+    )(operator_rows, spectra[0])
     if len(spectra) == 1:
         return own
     terms = pl.pallas_call(
@@ -155,7 +168,7 @@
         scratch_shapes=[pltpu.VMEM(shape, jnp.float32)],
         compiler_params=pltpu.CompilerParams(vmem_limit_bytes=SCOPED),
         name="other_products",
-    )(place, weights, in_fast(own), *spectra[1:])
+    )(place, in_fast(weights), in_fast(own), *spectra[1:])
     return terms.reshape((len(spectra) * series_count,) + shape[1:])
 
 
@@ -163,12 +176,15 @@
     total = lax.axis_size("param")
     member = lax.axis_index("param") // stride % count
     moved = []
+    mirrored = count & (count - 1) == 0
     for step in range(1, count):
         pairs = []
         for source in range(total):
             place = source // stride % count
-            pairs.append((source, source + ((place + step) % count - place) * stride))
-        chunk = lax.dynamic_index_in_dim(terms, (member + step) % count, 0, keepdims=False)
+            target = place ^ step if mirrored else (place + step) % count
+            pairs.append((source, source + (target - place) * stride))
+        target = member ^ step if mirrored else (member + step) % count
+        chunk = lax.dynamic_index_in_dim(terms, target, 0, keepdims=False)
         moved.append(lax.ppermute(chunk.astype(jnp.bfloat16), "param", pairs))
     result = lax.dynamic_index_in_dim(terms, member, 0, keepdims=False).astype(jnp.float32)
     for one in moved:

time: 31.3 us -> 28.4 us (0.907)
  waiting for transfers between devices: 11.5 us -> 8.17 us
  Pallas kernels: 4.26 us -> 6.81 us
  local copies, waits for them, and re-layouts: 1.77 us -> 0.05 us
    pallas_call x1, Pallas kernels: 1.04 us -> 2.94 us  [products(): pl.pallas_call(own_kernel, in_specs=[pl.BlockSpec(memory_space=pl.ANY), i...]
    ppermute x2, waiting for transfers between devices: 3.88 us -> 2.13 us  [exchange(): moved.append(lax.ppermute(own, axis, pairs))]
    unnamed x8 -> x6, local copies, waits for them, and re-layouts: 1.74 us -> 0.01 us
    ppermute x6, waiting for transfers between devices: 7.62 us -> 6.04 us  [scatter_sum(): moved.append(lax.ppermute(chunk.astype(jnp.bfloat16), 'param', pairs))]
    pallas_call x1, Pallas kernels: 2.18 us -> 2.82 us  [transform(): pl.pallas_call(transform_kernel, in_specs=[pl.BlockSpec(memory_space=pltp...]
    ppermute x6, starting transfers between devices: 6.74 us -> 6.37 us  [scatter_sum(): moved.append(lax.ppermute(chunk.astype(jnp.bfloat16), 'param', pairs))]
  transfers between devices with their start and end apart: 8 -> 8, of which waited for: 7 -> 5; matrix products, arithmetic and copies ran while one was open for 0% -> 0% of each run, Pallas kernels for 3% -> 10%
where the time goes in v3:
time: 28.4 us; the launch traced here: 28.3 us
  starting transfers between devices  11 us (39%)
  waiting for transfers between devices  8.17 us (29%)
  Pallas kernels  6.81 us (24%)
  between operations  1.52 us (5%)
  other arithmetic  0.63 us (2%)
    ppermute x6, starting transfers between devices, scatter_sum(): moved.append(lax.ppermute(chunk.astype(jnp.bfloat16), 'param', pairs))  6.37 us
    ppermute x6, waiting for transfers between devices, scatter_sum(): moved.append(lax.ppermute(chunk.astype(jnp.bfloat16), 'param', pairs))  6.04 us
    ppermute x2, starting transfers between devices, exchange(): moved.append(lax.ppermute(own, axis, pairs))  4.6 us
    pallas_call x1, Pallas kernels, products(): pl.pallas_call(own_kernel, in_specs=[pl.BlockSpec(memory_space=pl.ANY), i...  2.94 us
    pallas_call x1, Pallas kernels, transform(): pl.pallas_call(transform_kernel, in_specs=[pl.BlockSpec(memory_space=pltp...  2.82 us
    ppermute x2, waiting for transfers between devices, exchange(): moved.append(lax.ppermute(own, axis, pairs))  2.13 us
    pallas_call x1, Pallas kernels, products(): pl.pallas_call(other_kernel, in_specs=[pl.BlockSpec(memory_space=pltpu.SM...  1.05 us
    mul x1, other arithmetic, local(): return (qoi_spectrum, summed * norm_factor)  0.6 us
  transfers between devices with their start and end apart: 8, of which 5 were waited for; matrix products, arithmetic and copies ran while one was open for 0% of the time, Pallas kernels for 10%

profile of v3, /device:TPU:0, one launch (start us, length us, event | category | flops | bytes accessed | tf_op | source)
XLA Modules:
  0.0 28.3 jit_solution(8298660986120216710)
XLA Ops:
  0.6 0.0 copy-start
  1.4 2.8 %transform.1.spectrum_ref = bf16[128,320]{1,0:T(8,128)(2,1)S(1)} custom-call(s32[1]{0:T(128)S(6)} %copy.7.start_ref, bf16[3360,320]{1,0:T(8,128)(2,1)} %bitcast.38), custom_call_target="tpu_custom_call" | custom-call | tf_op jit(solution)/shard_map/transform/pallas_call | solution.py:70
  4.3 3.1 %collective-permute-start = (bf16[128,320]{1,0:T(8,128)(2,1)S(1)}, bf16[128,320]{1,0:T(8,128)(2,1)S(1)}, u32[]{:S(2)}, u32[]{:S(2)}) collective-permute-start(bf16[128,320]{1,0:T(8,128)(2,1)S(1)} %transform.1.spectrum_ref), channel_id=1, source_target_pairs={{0,1},{1,0},{2,3},{3,2},{4,5},{5,4},{6,7},{7,6},{8,9},{9,8},{10,11... | collective-permute-start | bytes 245768 | tf_op jit(solution)/shard_map/ppermute | solution.py:134
  7.3 0.0 copy-done
  7.3 0.0 copy-start.2
  7.3 2.9 %own_products.1 = (bf16[8,2,8,256]{3,2,1,0:T(8,128)(2,1)S(1)}, bf16[8,320,2,256]{3,2,1,0:T(2,128)(2,1)S(1)}) custom-call(bf16[8,320,2,256]{3,2,1,0:T(2,128)(2,1)S(1)} %copy-done, bf16[128,320]{1,0:T(8,128)(2,1)S(1)} %transform.1.spectrum_ref), custom_call_target="tpu_custom_call" | custom-call | flops 335544320 | bytes 1310720 | tf_op jit(solution)/shard_map/own_products/pallas_call | solution.py:150
  10.3 0.0 collective-permute-done.refs_0_
  10.3 1.0 %other_products.1 = bf16[2,8,2,8,256]{4,3,2,1,0:T(8,128)(2,1)S(1)} custom-call(s32[1]{0:T(128)} %bitcast.place_ref, bf16[8,320,2,256]{3,2,1,0:T(2,128)(2,1)S(1)} %get-tuple-element.4.weights_ref, bf16[8,2,8,256]{3,2,1,0:T(8,128)(2,1)S(1)} %get-tuple-element.5.own_ref, bf16[128,320]{1,0:T(8,128)(2,1)S(1)} %collective-permute-done.refs_0_), custom_call_target="tpu_custom_call" | custom-call | tf_op jit(solution)/shard_map/other_products/pallas_call | solution.py:164
  11.4 3.8 %collective-permute-start.3 = (bf16[4,1,2,8,256]{4,3,2,1,0:T(8,128)(2,1)S(1)}, bf16[4,1,2,8,256]{4,3,2,1,0:T(8,128)(2,1)S(1)}, u32[]{:S(2)}, u32[]{:S(2)}) collective-permute-start(bf16[4,1,2,8,256]{4,3,2,1,0:T(8,128)(2,1)S(1)} %get-tuple-element.8), channel_id=1, source_target_pairs={{0,24},{2,26},{4,28},{6,30},{8,16},{10,18},{12,20},{14,22},{16,8},... | collective-permute-start | bytes 98312 | tf_op jit(solution)/shard_map/ppermute | solution.py:188
  15.2 0.0 collective-permute-start.2
  15.2 0.6 %collective-permute-start.1 = (bf16[4,1,2,8,256]{4,3,2,1,0:T(8,128)(2,1)S(1)}, bf16[4,1,2,8,256]{4,3,2,1,0:T(8,128)(2,1)S(1)}, u32[]{:S(2)}, u32[]{:S(2)}) collective-permute-start(bf16[4,1,2,8,256]{4,3,2,1,0:T(8,128)(2,1)S(1)} %get-tuple-element.6), channel_id=1, source_target_pairs={{0,8},{2,10},{4,12},{6,14},{8,0},{10,2},{12,4},{14,6},{16,24},{18,... | collective-permute-start | bytes 98312 | tf_op jit(solution)/shard_map/ppermute | solution.py:188
  15.8 1.7 %collective-permute-done.3 = bf16[4,1,2,8,256]{4,3,2,1,0:T(8,128)(2,1)S(1)} collective-permute-done((bf16[4,1,2,8,256]{4,3,2,1,0:T(8,128)(2,1)S(1)}, bf16[4,1,2,8,256]{4,3,2,1,0:T(8,128)(2,1)S(1)}, u32[]{:S(2)}, u32[]{:S(2)}) %collective-permute-start.3) | collective-permute-done | bytes 32800 | tf_op jit(solution)/shard_map/ppermute | solution.py:188
  17.5 2.5 %collective-permute-done.2 = bf16[4,1,2,8,256]{4,3,2,1,0:T(8,128)(2,1)S(1)} collective-permute-done((bf16[4,1,2,8,256]{4,3,2,1,0:T(8,128)(2,1)S(1)}, bf16[4,1,2,8,256]{4,3,2,1,0:T(8,128)(2,1)S(1)}, u32[]{:S(2)}, u32[]{:S(2)}) %collective-permute-start.2) | collective-permute-done | bytes 32800 | tf_op jit(solution)/shard_map/ppermute | solution.py:188
  20.0 0.0 collective-permute-done.1
  20.0 0.1 collective-permute-start.6
  20.1 1.6 %collective-permute-start.5 = (bf16[1,2,8,256]{3,2,1,0:T(8,128)(2,1)S(1)}, bf16[1,2,8,256]{3,2,1,0:T(8,128)(2,1)S(1)}, u32[]{:S(2)}, u32[]{:S(2)}) collective-permute-start(bf16[1,2,8,256]{3,2,1,0:T(8,128)(2,1)S(1)} %get-tuple-element.11), channel_id=1, source_target_pairs={{0,4},{2,6},{4,0},{6,2},{8,12},{10,14},{12,8},{14,10},{16,20},{18,... | collective-permute-start | bytes 24584 | tf_op jit(solution)/shard_map/ppermute | solution.py:188
  21.7 0.3 %collective-permute-start.4 = (bf16[1,2,8,256]{3,2,1,0:T(8,128)(2,1)S(1)}, bf16[1,2,8,256]{3,2,1,0:T(8,128)(2,1)S(1)}, u32[]{:S(2)}, u32[]{:S(2)}) collective-permute-start(bf16[1,2,8,256]{3,2,1,0:T(8,128)(2,1)S(1)} %get-tuple-element.9), channel_id=1, source_target_pairs={{0,2},{2,0},{4,6},{6,4},{8,10},{10,8},{12,14},{14,12},{16,18},{18,... | collective-permute-start | bytes 24584 | tf_op jit(solution)/shard_map/ppermute | solution.py:188
  22.0 1.3 %collective-permute-done.6 = bf16[1,2,8,256]{3,2,1,0:T(8,128)(2,1)S(1)} collective-permute-done((bf16[1,2,8,256]{3,2,1,0:T(8,128)(2,1)S(1)}, bf16[1,2,8,256]{3,2,1,0:T(8,128)(2,1)S(1)}, u32[]{:S(2)}, u32[]{:S(2)}) %collective-permute-start.6) | collective-permute-done | bytes 8224 | tf_op jit(solution)/shard_map/ppermute | solution.py:188
  23.2 0.6 %collective-permute-done.5 = bf16[1,2,8,256]{3,2,1,0:T(8,128)(2,1)S(1)} collective-permute-done((bf16[1,2,8,256]{3,2,1,0:T(8,128)(2,1)S(1)}, bf16[1,2,8,256]{3,2,1,0:T(8,128)(2,1)S(1)}, u32[]{:S(2)}, u32[]{:S(2)}) %collective-permute-start.5) | collective-permute-done | bytes 8224 | tf_op jit(solution)/shard_map/ppermute | solution.py:188
  23.8 0.0 collective-permute-done.4
  23.8 0.0 copy-done.2
  23.9 0.0 copy-start.1
  23.9 0.1 convolution_bitcast_fusion
  24.0 1.5 %collective-permute-start.7 = (f32[1,2,8,16]{3,2,1,0:T(8,128)S(1)}, f32[1,2,8,16]{3,2,1,0:T(8,128)S(1)}, u32[]{:S(2)}, u32[]{:S(2)}) collective-permute-start(f32[1,2,8,16]{3,2,1,0:T(8,128)S(1)} %convolution_bitcast_fusion), channel_id=1, source_target_pairs={{0,1},{1,0},{2,3},{3,2},{4,5},{5,4},{6,7},{7,6},{8,9},{9,8},{10,11... | collective-permute-start | bytes 3080 | tf_op jit(solution)/shard_map/ppermute | solution.py:134
  25.5 2.1 %collective-permute-done.7 = f32[1,2,8,16]{3,2,1,0:T(8,128)S(1)} collective-permute-done((f32[1,2,8,16]{3,2,1,0:T(8,128)S(1)}, f32[1,2,8,16]{3,2,1,0:T(8,128)S(1)}, u32[]{:S(2)}, u32[]{:S(2)}) %collective-permute-start.7) | collective-permute-done | bytes 1056 | tf_op jit(solution)/shard_map/ppermute | solution.py:134
  27.7 0.6 %add_multiply_fusion = f32[1,2,8,16]{3,2,1,0:T(8,128)} fusion(f32[1,2,8,16]{3,2,1,0:T(8,128)S(1)} %convolution_bitcast_fusion, f32[1,2,8,16]{3,2,1,0:T(8,128)S(1)} %collective-permute-done.7), kind=kLoop, calls=%fused_computation.19 | loop fusion | flops 512 | bytes 3072 | tf_op jit(solution)/shard_map/mul | solution.py:218
  28.3 0.0 copy-done.1
  (4 shorter events, 0.1 us)
Async XLA Ops:
  0.6 6.7 %copy-start = (bf16[8,320,2,256]{3,2,1,0:T(2,128)(2,1)S(1)}, bf16[8,320,2,256]{3,2,1,0:T(2,128)(2,1)}, u32[]{:S(2)}) copy-start(bf16[8,320,2,256]{3,2,1,0:T(2,128)(2,1)} %weights_ref.1) | copy-start | bytes 7864324
  4.3 6.0 %collective-permute-start = (bf16[128,320]{1,0:T(8,128)(2,1)S(1)}, bf16[128,320]{1,0:T(8,128)(2,1)S(1)}, u32[]{:S(2)}, u32[]{:S(2)}) collective-permute-start(bf16[128,320]{1,0:T(8,128)(2,1)S(1)} %transform.1.spectrum_ref), channel_id=1, source_target_pairs={{0,1},{1,0},{2,3},{3,2},{4,5},{5,4},{6,7},{7,6},{8,9},{9,8},{10,11... | collective-permute-start | bytes 245768 | tf_op jit(solution)/shard_map/ppermute | solution.py:134
  7.3 16.5 %copy-start.2 = (s32[256]{0:T(256)S(1)}, s32[256]{0:T(256)}, u32[]{:S(2)}) copy-start(s32[256]{0:T(256)} %param.7) | copy-start | bytes 3076
  11.4 6.1 %collective-permute-start.3 = (bf16[4,1,2,8,256]{4,3,2,1,0:T(8,128)(2,1)S(1)}, bf16[4,1,2,8,256]{4,3,2,1,0:T(8,128)(2,1)S(1)}, u32[]{:S(2)}, u32[]{:S(2)}) collective-permute-start(bf16[4,1,2,8,256]{4,3,2,1,0:T(8,128)(2,1)S(1)} %get-tuple-element.8), channel_id=1, source_target_pairs={{0,24},{2,26},{4,28},{6,30},{8,16},{10,18},{12,20},{14,22},{16,8},... | collective-permute-start | bytes 98312 | tf_op jit(solution)/shard_map/ppermute | solution.py:188
  15.2 4.8 %collective-permute-start.2 = (bf16[4,1,2,8,256]{4,3,2,1,0:T(8,128)(2,1)S(1)}, bf16[4,1,2,8,256]{4,3,2,1,0:T(8,128)(2,1)S(1)}, u32[]{:S(2)}, u32[]{:S(2)}) collective-permute-start(bf16[4,1,2,8,256]{4,3,2,1,0:T(8,128)(2,1)S(1)} %get-tuple-element.7), channel_id=1, source_target_pairs={{0,16},{2,18},{4,20},{6,22},{8,24},{10,26},{12,28},{14,30},{16,0},... | collective-permute-start | bytes 98312 | tf_op jit(solution)/shard_map/ppermute | solution.py:188
  15.2 4.8 %collective-permute-start.1 = (bf16[4,1,2,8,256]{4,3,2,1,0:T(8,128)(2,1)S(1)}, bf16[4,1,2,8,256]{4,3,2,1,0:T(8,128)(2,1)S(1)}, u32[]{:S(2)}, u32[]{:S(2)}) collective-permute-start(bf16[4,1,2,8,256]{4,3,2,1,0:T(8,128)(2,1)S(1)} %get-tuple-element.6), channel_id=1, source_target_pairs={{0,8},{2,10},{4,12},{6,14},{8,0},{10,2},{12,4},{14,6},{16,24},{18,... | collective-permute-start | bytes 98312 | tf_op jit(solution)/shard_map/ppermute | solution.py:188
  20.0 3.2 %collective-permute-start.6 = (bf16[1,2,8,256]{3,2,1,0:T(8,128)(2,1)S(1)}, bf16[1,2,8,256]{3,2,1,0:T(8,128)(2,1)S(1)}, u32[]{:S(2)}, u32[]{:S(2)}) collective-permute-start(bf16[1,2,8,256]{3,2,1,0:T(8,128)(2,1)S(1)} %get-tuple-element.10), channel_id=1, source_target_pairs={{0,6},{2,4},{4,2},{6,0},{8,14},{10,12},{12,10},{14,8},{16,22},{18,... | collective-permute-start | bytes 24584 | tf_op jit(solution)/shard_map/ppermute | solution.py:188
  20.1 3.7 %collective-permute-start.5 = (bf16[1,2,8,256]{3,2,1,0:T(8,128)(2,1)S(1)}, bf16[1,2,8,256]{3,2,1,0:T(8,128)(2,1)S(1)}, u32[]{:S(2)}, u32[]{:S(2)}) collective-permute-start(bf16[1,2,8,256]{3,2,1,0:T(8,128)(2,1)S(1)} %get-tuple-element.11), channel_id=1, source_target_pairs={{0,4},{2,6},{4,0},{6,2},{8,12},{10,14},{12,8},{14,10},{16,20},{18,... | collective-permute-start | bytes 24584 | tf_op jit(solution)/shard_map/ppermute | solution.py:188
  21.7 2.2 %collective-permute-start.4 = (bf16[1,2,8,256]{3,2,1,0:T(8,128)(2,1)S(1)}, bf16[1,2,8,256]{3,2,1,0:T(8,128)(2,1)S(1)}, u32[]{:S(2)}, u32[]{:S(2)}) collective-permute-start(bf16[1,2,8,256]{3,2,1,0:T(8,128)(2,1)S(1)} %get-tuple-element.9), channel_id=1, source_target_pairs={{0,2},{2,0},{4,6},{6,4},{8,10},{10,8},{12,14},{14,12},{16,18},{18,... | collective-permute-start | bytes 24584 | tf_op jit(solution)/shard_map/ppermute | solution.py:188
  23.9 4.4 %copy-start.1 = (f32[1,2,8,256]{3,2,1,0:T(8,128)}, f32[1,2,8,256]{3,2,1,0:T(8,128)S(1)}, u32[]{:S(2)}) copy-start(f32[1,2,8,256]{3,2,1,0:T(8,128)S(1)} %fusion.4) | copy-start | bytes 49156
  24.0 3.7 %collective-permute-start.7 = (f32[1,2,8,16]{3,2,1,0:T(8,128)S(1)}, f32[1,2,8,16]{3,2,1,0:T(8,128)S(1)}, u32[]{:S(2)}, u32[]{:S(2)}) collective-permute-start(f32[1,2,8,16]{3,2,1,0:T(8,128)S(1)} %convolution_bitcast_fusion), channel_id=1, source_target_pairs={{0,1},{1,0},{2,3},{3,2},{4,5},{5,4},{6,7},{7,6},{8,9},{9,8},{10,11... | collective-permute-start | bytes 3080 | tf_op jit(solution)/shard_map/ppermute | solution.py:134
